TPU v7x, 32 devices: a whole 2x2x4 slice. The times are simulated.
32 devices in a mesh: tp: 4 (over z), dp: 8 (over y, x, core).
Axes of the slice: x: 2, y: 2, z: 4, core: 2. Of those that a mesh axis runs over, the one named last changes fastest.
Arguments:
- design: float32 [49152, 2560], P('dp', 'tp')
- target: float32 [49152], P('dp')
- ridge: float32 [], replicated
Outputs:
- output 1: float32 [2560], replicated
- output 2: float32 [49152], P('dp')
All inputs are finite; a program needn't handle non-finite values.
Results may differ from a plain program's by a relative error of at most 0.001.
Values sent between devices are 32-bit elements.
A program may use at most 1 GiB of HBM per device.

v0:
```python
import jax
import jax.numpy as jnp
from jax import lax
from jax.sharding import PartitionSpec as P

HIGHEST = lax.Precision.HIGHEST
CONTRACT_ROWS = (((0,), (0,)), ((), ()))


def solve_factored(chol_low, rhs_vec):
    half_solve = lax.linalg.triangular_solve(chol_low, rhs_vec[:, None], left_side=True, lower=True)
    return lax.linalg.triangular_solve(chol_low, half_solve, left_side=True, lower=True, transpose_a=True)[:, 0]


def solution(mesh):
    col_ways = mesh.shape['tp']

    def local_fit(design_blk, target_blk, ridge):
        rows_dev, cols_dev = design_blk.shape
        features = cols_dev * col_ways
        sub_rows = rows_dev // col_ways
        col_index = lax.axis_index('tp')
        row_panel = lax.all_to_all(design_blk, 'tp', 0, 1, tiled=True)
        target_part = lax.dynamic_slice_in_dim(target_blk, col_index * sub_rows, sub_rows)
        gram_part = lax.dot_general(row_panel, row_panel, CONTRACT_ROWS, precision=HIGHEST, preferred_element_type=jnp.float32)
        moment_part = lax.dot_general(row_panel, target_part, CONTRACT_ROWS, precision=HIGHEST, preferred_element_type=jnp.float32)
        gram_mat = lax.psum(gram_part, ('tp', 'dp'))
        moment_vec = lax.psum(moment_part, ('tp', 'dp'))
        chol_low = jnp.linalg.cholesky(gram_mat + ridge * jnp.eye(features, dtype=jnp.float32))
        coeffs = solve_factored(chol_low, moment_vec)
        coeff_blk = lax.dynamic_slice_in_dim(coeffs, col_index * cols_dev, cols_dev)
        part_fit = jnp.dot(design_blk, coeff_blk, precision=HIGHEST, preferred_element_type=jnp.float32)
        fitted = lax.psum(part_fit, 'tp')
        return coeffs, target_blk - fitted

    return jax.shard_map(local_fit, mesh=mesh, in_specs=(P('dp', 'tp'), P('dp'), P()), out_specs=(P(), P('dp')), check_vma=False)
```

profile of v0, /device:TPU:0, one launch (start us, length us, event | category | flops | bytes accessed | tf_op | source)
XLA Modules:
  0.0 2095.3 jit_solution(8836155051508011915)
XLA Ops:
  7.2 352.6 %all_to_all.19 = f32[4,1536,640]{2,1,0:T(8,128)} all-to-all(f32[4,1536,640]{2,1,0:T(8,128)} %bitcast.965), channel_id=1, replica_groups=mesh['tp'=4,'dp'=8] {'tp'}, dimensions={0} | all-to-all | bytes 31457280 | tf_op jit(solution)/shard_map/all_to_all | solution.py:23
  359.8 15.6 copy.89
  375.5 133.5 %fusion.365 = f32[2560,2560]{0,1:T(8,128)} fusion(f32[1536,2560]{0,1:T(8,128)} %bitcast.966), kind=kOutput, calls=%fused_computation.859 | convolution fusion | flops 120795955200 | bytes 41943040 | tf_op jit(solution)/shard_map/dot_general | solution.py:25
  509.8 15.5 convolution_reduce_fusion
  525.3 43.4 %psum.22 = f32[2560]{0:T(1024)S(1)} all-reduce(f32[2560]{0:T(1024)S(1)} %convolution_reduce_fusion), channel_id=1, replica_groups=mesh['tp'=4,'dp'=8] {'tp','dp'}, use_global_device_ids=true, to_apply=%region_41.42 | all-reduce | flops 2560 | bytes 20480 | tf_op jit(solution)/shard_map/psum | solution.py:28
  568.6 347.6 %all-reduce.3.cloned.1.call-done = f32[2560,2560]{0,1:T(8,128)} async-done(((f32[2560,2560]{0,1:T(8,128)}), f32[2560,2560]{0,1:T(8,128)}) %all-reduce.3.cloned.1.call-update) | async-done | bytes 26214416 | tf_op jit(solution)/shard_map/psum | solution.py:27
  916.2 18.4 select_add_fusion
  934.6 27.3 %copy.91 = f32[2560,2560]{1,0:T(8,128)} copy(f32[2560,2560]{0,1:T(8,128)} %select_add_fusion) | data formatting | bytes 52428800 | tf_op jit(solution)/shard_map/add | solution.py:29
  961.9 17.1 fusion
  1092.9 12.1 cholesky.641
  1186.6 12.1 fusion.45
  1223.1 12.5 fusion.42
  1259.9 12.6 fusion.39
  1296.7 13.6 fusion.36
  1334.2 13.1 fusion.33
  1371.2 13.8 fusion.30
  1408.7 12.7 fusion.65
  1445.2 12.7 fusion.68
  1592.7 12.1 cholesky.1448
  1687.2 18.6 select_select_fusion
  1705.8 74.6 %while.1 = (s32[]{:T(128)}, f32[2560,2560]{0,1:T(8,128)}, s32[20,2]{0,1:T(2,128)S(1)}, f32[20,128,128]{2,1,0:T(8,128)}, s32[]{:T(128)}) while((s32[]{:T(128)}, f32[2560,2560]{0,1:T(8,128)}, s32[20,2]{0,1:T(2,128)S(1)}, f32[20,128,128]{2,1,0:T(8,128)}, s32[]{:T(128)}) %tuple.241), condition=%wide.while_cond, body=%wide.while_body.sunk | while | flops 2 | bytes 393329 | solution.py:12
  1780.4 197.4 %custom-call.179 = f32[20,128,128]{1,2,0:T(8,128)S(1)} custom-call(f32[20,128,128]{2,1,0:T(8,128)} %get-tuple-element.9), custom_call_target="InvertDiagBlocksLowerTriangular" | custom-call | tf_op jit(solution)/shard_map/triangular_solve | solution.py:12
  2051.6 18.4 fusion.324
  2070.0 17.6 psum.23
  (544 shorter events, 716.0 us)
Async XLA Ops:
  7.2 909.0 %all-reduce.3.cloned.1.call-start = ((), (), s32[]{:S(2)}) async-start(), calls=%async_computation.1 | async-start | bytes 52428800 | tf_op jit(solution)/shard_map/psum | solution.py:27
  508.9 0.7 copy-start.2
  979.0 8.6 copy-start
  1015.7 36.5 %copy-start.1 = (f32[2432,128]{1,0:T(8,128)S(1)}, f32[2432,128]{1,0:T(8,128)}, u32[]{:S(2)}) copy-start(f32[2432,128]{1,0:T(8,128)} %convolution_subtract_fusion.2) | copy-start | bytes 3735556
Sparse Core Ops, SparseCore 0:
  509.1 407.0 all-reduce.2
where the time goes:
time: 2110 us; the launch traced here: 2100 us
  other arithmetic  689 us (33%)
  matrix products  459 us (22%)
  blocking collectives  414 us (20%)
  waiting for transfers between devices  348 us (16%)
  local copies, waits for them, and re-layouts  157 us (7%)
  between operations  28.7 us (1%)
    another operation x78, other arithmetic, local_fit(): jnp.linalg.cholesky(gram_mat + ridge * jnp.eye(features, dtype=jnp.float32))  436 us
    all_to_all x1, blocking collectives, local_fit(): row_panel = lax.all_to_all(design_blk, 'tp', 0, 1, tiled=True)  353 us
    psum x1, waiting for transfers between devices, local_fit(): gram_mat = lax.psum(gram_part, ('tp', 'dp'))  348 us
    another operation x38, matrix products, local_fit(): jnp.linalg.cholesky(gram_mat + ridge * jnp.eye(features, dtype=jnp.float32))  222 us
    another operation x4, other arithmetic, solve_factored(): lax.linalg.triangular_solve(chol_low, half_solve, left_side=True, lower=T...  217 us
    dot_general x1, matrix products, local_fit(): lax.dot_general(row_panel, row_panel, CONTRACT_ROWS, precision=HIGHEST, p...  133 us
    another operation x100, local copies, waits for them, and re-layouts  74.4 us
    psum x1, blocking collectives, local_fit(): moment_vec = lax.psum(moment_part, ('tp', 'dp'))  43.4 us
  transfers between devices with their start and end apart: 1, of which 1 were waited for; matrix products, arithmetic and copies ran while one was open for 1% of the time, Pallas kernels for 0%

commit v1 on v0

v1 whole, which is shorter than its diff:
```python
import functools

import jax
import jax.numpy as jnp
from jax import lax
from jax.experimental import pallas as pl
from jax.experimental.pallas import tpu as pltpu
from jax.sharding import PartitionSpec as P


LANES = 128
SUB = 8
BLK = 128
NB = 512
F32 = jnp.float32
BF16 = jnp.bfloat16


def split3(x):
    hi = x.astype(BF16)
    rest = x - hi.astype(F32)
    mid = rest.astype(BF16)
    low = (rest - mid.astype(F32)).astype(BF16)
    return hi, mid, low


def lhs_cat(x):
    hi, mid, low = split3(x)
    return jnp.concatenate([hi, mid, hi, low, mid, hi], axis=1)


def rhs_cat(x):
    hi, mid, low = split3(x)
    return jnp.concatenate([mid, hi, low, hi, mid, hi], axis=0)


def dot_cat(lhs, rhs):
    return lax.dot_general(lhs, rhs, (((1,), (0,)), ((), ())), preferred_element_type=F32)


def row_sums(parts, sub):
    for shift in (4, 2, 1):
        low = (sub & shift) == 0
        nxt = []
        for t in range(shift):
            a, b = parts[t], parts[t + shift]
            keep = jnp.where(low, a, b)
            move = jnp.where(low, b, a)
            nxt.append(keep + xor_roll(move, shift, sub))
        parts = nxt
    return parts[0]


def xor_roll(x, shift, sub):
    if shift == 4:
        return pltpu.roll(x, 4, 0)
    low = (sub & shift) == 0
    return jnp.where(low, pltpu.roll(x, SUB - shift, 0), pltpu.roll(x, shift, 0))


def bcast_lane(x, c):
    return jnp.broadcast_to(x[:, c:c + 1], (SUB, LANES))


def bcast_row(x, p):
    return jnp.broadcast_to(x[p:p + 1, :], (SUB, LANES))


def factor_block(load, sub, lane):
    octs = BLK // SUB
    a = [load(o) for o in range(octs)]
    e = [jnp.where(lane == sub + SUB * o, 1.0, 0.0).astype(F32) for o in range(octs)]
    out = [None] * octs
    for t in range(octs // 2):
        o0, o1 = 2 * t, 2 * t + 1
        c0 = 16 * t
        r0, r1, e0, e1 = a[o0], a[o1], e[o0], e[o1]
        b0 = [bcast_lane(r0, c0 + q) for q in range(16)]
        b1 = [bcast_lane(r1, c0 + q) for q in range(16)]
        d0 = jnp.ones((SUB, LANES), F32)
        d1 = jnp.ones((SUB, LANES), F32)
        for p in range(16):
            ps = p % 8
            first = p < 8
            piv = bcast_row(b0[p] if first else b1[p], ps)
            inv = 1.0 / piv
            if first:
                d0 = jnp.where(sub == ps, piv, d0)
                m0 = jnp.where(sub > ps, b0[p] * inv, 0.0)
                m1 = b1[p] * inv
            else:
                d1 = jnp.where(sub == ps, piv, d1)
                m1 = jnp.where(sub > ps, b1[p] * inv, 0.0)
            for q in range(p + 1, 16):
                row = bcast_row(b0[q] if first else b1[q], ps)
                if first and ps < 7:
                    b0[q] = b0[q] - m0 * row
                b1[q] = b1[q] - m1 * row
            rr, re = bcast_row(r0 if first else r1, ps), bcast_row(e0 if first else e1, ps)
            if first and ps < 7:
                r0 = r0 - m0 * rr
                e0 = e0 - m0 * re
            r1 = r1 - m1 * rr
            e1 = e1 - m1 * re
        s0, s1 = lax.rsqrt(d0), lax.rsqrt(d1)
        u0, u1, v0, v1 = r0 * s0, r1 * s1, e0 * s0, e1 * s1
        out[o0], out[o1] = v0, v1
        for o in range(2 * t + 2, octs):
            xs, ys = [], []
            for k in range(SUB):
                i = SUB * o + k
                g0, g1 = bcast_lane(u0, i), bcast_lane(u1, i)
                xs.append(g0 * u0 + g1 * u1)
                ys.append(g0 * v0 + g1 * v1)
            a[o] = a[o] - row_sums(xs, sub)
            e[o] = e[o] - row_sums(ys, sub)
    return out


def diag_kernel(lam_ref, s_ref, w_ref, work):
    n = s_ref.shape[0]
    steps = n // BLK
    sub = lax.broadcasted_iota(jnp.int32, (SUB, LANES), 0)
    lane = lax.broadcasted_iota(jnp.int32, (SUB, LANES), 1)
    row = lax.broadcasted_iota(jnp.int32, (n, n), 0)
    col = lax.broadcasted_iota(jnp.int32, (n, n), 1)
    work[:, :n] = s_ref[...] + jnp.where(row == col, lam_ref[0], 0.0)
    work[:, n:] = jnp.where(row == col, 1.0, 0.0)

    def step(k, carry):
        base = pl.multiple_of(k * BLK, BLK)
        win = pl.ds(pl.multiple_of(base + BLK, BLK), n)
        diag = pl.ds(base, BLK)

        def load(o):
            return work[pl.ds(pl.multiple_of(base + SUB * o, SUB), SUB), diag]

        inv = jnp.concatenate(factor_block(load, sub, lane), axis=0)
        panel = dot_cat(lhs_cat(inv), rhs_cat(work[diag, win]))
        work[diag, win] = panel
        right = rhs_cat(panel)
        for j in range(steps - 1):
            @pl.when(k == j)
            def _(j=j):
                rows = n - BLK * (j + 1)
                left = lhs_cat(panel[:, :rows].T)
                w = (pl.ds(BLK * (j + 1), rows), pl.ds(BLK * (j + 1), n))
                work[w] = work[w] - dot_cat(left, right)
        return carry

    lax.fori_loop(0, steps, step, 0)
    w_ref[...] = work[:, n:]


def diag_inverse(sdiag, lam):
    n = sdiag.shape[0]
    return pl.pallas_call(
        diag_kernel,
        out_shape=jax.ShapeDtypeStruct((n, n), F32),
        in_specs=[pl.BlockSpec(memory_space=pltpu.SMEM), pl.BlockSpec(memory_space=pltpu.VMEM)],
        out_specs=pl.BlockSpec(memory_space=pltpu.VMEM),
        scratch_shapes=[pltpu.VMEM((n, 2 * n), F32)],
        cost_estimate=pl.CostEstimate(flops=20_000_000_000, bytes_accessed=8 * n * n, transcendentals=0),
        name="diag_inverse",
    )(lam.reshape(1), sdiag)


def solve_kernel(n, h_ref, *refs):
    pairs = [(j, c) for c in range(n) for j in range(c)]
    u_refs = dict(zip(pairs, refs[:len(pairs)]))
    w_refs = refs[len(pairs):len(pairs) + n]
    x_ref = refs[len(pairs) + n]
    half = []
    for c in range(n):
        right = h_ref[c:c + 1, :]
        for j in range(c):
            right = right - jnp.sum(u_refs[j, c][...] * half[j], axis=0, keepdims=True)
        half.append(jnp.sum(w_refs[c][...] * right, axis=1, keepdims=True))
    for c in reversed(range(n)):
        left = half[c]
        for k in range(c + 1, n):
            left = left - jnp.sum(u_refs[c, k][...] * x_ref[k:k + 1, :], axis=1, keepdims=True)
        x_ref[c:c + 1, :] = jnp.sum(w_refs[c][...] * left, axis=0, keepdims=True)


def solve(moment, uppers, inverses):
    n = len(inverses)
    blocks = [uppers[j, c] for c in range(n) for j in range(c)]
    return pl.pallas_call(
        functools.partial(solve_kernel, n),
        out_shape=jax.ShapeDtypeStruct((n, NB), F32),
        in_specs=[pl.BlockSpec(memory_space=pltpu.VMEM)] * (1 + len(blocks) + n),
        out_specs=pl.BlockSpec(memory_space=pltpu.VMEM),
        compiler_params=pltpu.CompilerParams(vmem_limit_bytes=40 * 1024 * 1024),
        cost_estimate=pl.CostEstimate(flops=5_000_000_000, bytes_accessed=16_000_000, transcendentals=0),
        name="solve",
    )(moment, *blocks, *inverses)


HIGHEST = lax.Precision.HIGHEST
CONTRACT_ROWS = (((0,), (0,)), ((), ()))


def gram(left, right):
    return lax.dot_general(left, right, CONTRACT_ROWS, precision=HIGHEST, preferred_element_type=F32)


GROUPS = ((0, 1), (2,), (3,), (4,))


def swap(x, axis, ways, mask):
    return lax.ppermute(x, axis, [(i, i ^ mask) for i in range(ways)])


def pick(stack, i):
    return lax.dynamic_index_in_dim(stack, i, 0, keepdims=False)


def scatter_sum(x, me, ways, send):
    parts = x.reshape(ways, -1, x.shape[1])
    total = pick(parts, me)
    for m in range(1, ways):
        total = total + send(pick(parts, me ^ m), m)
    return total


def gather(x, me, ways, send):
    out = jnp.zeros((ways * x.shape[0], x.shape[1]), x.dtype)
    for m in range(ways):
        out = lax.dynamic_update_slice(out, send(x, m) if m else x, ((me ^ m) * x.shape[0], 0))
    return out


def sum_all(x, tp_ways, dp_ways):
    tp, dp = lax.axis_index('tp'), lax.axis_index('dp')
    core = (dp & 1, 2, lambda v, m: swap(v, 'dp', dp_ways, m))
    plane = (dp >> 1, dp_ways // 2, lambda v, m: swap(v, 'dp', dp_ways, 2 * m))
    column = (tp, tp_ways, lambda v, m: swap(v, 'tp', tp_ways, m))
    for level in (core, plane, column):
        x = scatter_sum(x, *level)
    part = x
    for level in (column, plane, core):
        x = gather(x, *level)
    return x, part


def solution(mesh):
    tp_ways, dp_ways = mesh.shape['tp'], mesh.shape['dp']

    def exchange(design_blk, tp, c, width, after):
        block = design_blk[:, width * c:width * (c + 1)].reshape(tp_ways, -1, width)
        if after is not None:
            block, _ = lax.optimization_barrier((block, after))
        got = [pick(block, tp)]
        for m in range(1, tp_ways):
            got.append(swap(pick(block, tp ^ m), 'tp', tp_ways, m))
        return got

    def local_fit(design_blk, target_blk, ridge):
        rows_dev, cols_dev = design_blk.shape
        sub_rows = rows_dev // tp_ways
        width = NB // tp_ways
        chunks = cols_dev // width
        tp = lax.axis_index('tp')
        target_part = lax.dynamic_slice_in_dim(target_blk, tp * sub_rows, sub_rows)
        target_pad = jnp.pad(target_part[:, None], ((0, 0), (0, SUB - 1)))

        got, cols, totals, uppers, inverses, moments = [], [], {}, {}, [], []
        for c in range(chunks):
            after = tuple(got[c - 2][1:]) if c >= 2 else None
            got.append(exchange(design_blk, tp, c, width, after))
            col = jnp.zeros((sub_rows, NB), F32)
            for m in range(tp_ways):
                col = lax.dynamic_update_slice(col, got[c][m], (0, (tp ^ m) * width))
            cols.append(col)
        part = None
        for group in GROUPS:
            parts = []
            for c in group:
                if part is not None:
                    cols[c], _ = lax.optimization_barrier((cols[c], part))
                blocks = [gram(cols[j], cols[c]) for j in range(c + 1)]
                moment = gram(target_pad, cols[c])[0]
                blocks[c] = lax.dynamic_update_slice(blocks[c], moment.reshape(2, NB // 2), (NB - 2, 0))
                parts += blocks
            total, part = sum_all(jnp.concatenate(parts, axis=0), tp_ways, dp_ways)
            row = 0
            for c in group:
                totals[c] = [total[row + NB * k:row + NB * (k + 1)] for k in range(c + 1)]
                row += NB * (c + 1)
            for c in group:
                moments.append(totals[c][c][-2:, :NB // 2].reshape(1, NB))
                for k in range(c + 1):
                    block = totals[c][k]
                    for j in range(k):
                        block = block - gram(uppers[j, k], uppers[j, c])
                    if k < c:
                        uppers[k, c] = jnp.dot(inverses[k], block, precision=HIGHEST, preferred_element_type=F32)
                    else:
                        inverses.append(diag_inverse(block, ridge))
        order = solve(jnp.concatenate(moments, axis=0), uppers, inverses)
        order = order.reshape(chunks, tp_ways, width)
        coeffs = order.transpose(1, 0, 2).reshape(-1)
        coeff_blk = lax.dynamic_index_in_dim(order, tp, 1, keepdims=False).reshape(-1)
        fitted = jnp.sum(design_blk * coeff_blk[None, :], axis=1)
        for k in range(tp_ways.bit_length() - 1):
            fitted = fitted + swap(fitted, 'tp', tp_ways, 1 << k)
        return coeffs, target_blk - fitted

    return jax.shard_map(local_fit, mesh=mesh, in_specs=(P('dp', 'tp'), P('dp'), P()), out_specs=(P(), P('dp')), check_vma=False)
```

time: 2110 us -> 986 us (0.47)
  other arithmetic: 689 us -> 22.1 us
  blocking collectives: 414 us -> 0 us
  matrix products: 459 us -> 234 us
  starting transfers between devices: 0.04 us -> 185 us
  Pallas kernels: 0 us -> 102 us
  waiting for transfers between devices: 348 us -> 306 us
  local copies, waits for them, and re-layouts: 157 us -> 126 us
  between operations: 28.7 us -> 3.2 us
    another operation x82 -> x0, other arithmetic: 653 us -> none  [the longest x78 436 us: local_fit(): jnp.linalg.cholesky(gram_mat + ridge * jnp.eye(features, dtype=jnp.float32))]
    all_to_all x1 -> x0, blocking collectives: 353 us -> none  [local_fit(): row_panel = lax.all_to_all(design_blk, 'tp', 0, 1, tiled=True)]
    psum x1 -> x0, waiting for transfers between devices: 348 us -> none  [local_fit(): gram_mat = lax.psum(gram_part, ('tp', 'dp'))]
    ppermute x0 -> x73, waiting for transfers between devices: none -> 306 us  [swap(): return lax.ppermute(x, axis, [(i, i ^ mask) for i in range(ways)])]
    another operation x116 -> x0, matrix products: 292 us -> none  [the longest x38 222 us: local_fit(): jnp.linalg.cholesky(gram_mat + ridge * jnp.eye(features, dtype=jnp.float32))]
    ppermute x0 -> x73, starting transfers between devices: none -> 185 us  [swap(): return lax.ppermute(x, axis, [(i, i ^ mask) for i in range(ways)])]
    pallas_call x0 -> x6, Pallas kernels: none -> 102 us  [the longest x5 97.9 us: diag_inverse(): pl.pallas_call(diag_kernel, out_shape=jax.ShapeDtypeStruct((n, n), F32),...]
    another operation x178 -> x16, local copies, waits for them, and re-layouts: 103 us -> 12.1 us
  transfers between devices with their start and end apart: 1 -> 73, of which waited for: 1 -> 33; matrix products, arithmetic and copies ran while one was open for 1% -> 26% of each run, Pallas kernels for 0% -> 8%
where the time goes in v1:
time: 986 us; the launch traced here: 977 us
  waiting for transfers between devices  306 us (31%)
  matrix products  234 us (24%)
  starting transfers between devices  185 us (19%)
  local copies, waits for them, and re-layouts  126 us (13%)
  Pallas kernels  102 us (10%)
  other arithmetic  22.1 us (2%)
    ppermute x73, waiting for transfers between devices, swap(): return lax.ppermute(x, axis, [(i, i ^ mask) for i in range(ways)])  306 us
    dot_general x40, matrix products, gram(): lax.dot_general(left, right, CONTRACT_ROWS, precision=HIGHEST, preferred_...  213 us
    ppermute x73, starting transfers between devices, swap(): return lax.ppermute(x, axis, [(i, i ^ mask) for i in range(ways)])  185 us
    pallas_call x5, Pallas kernels, diag_inverse(): pl.pallas_call(diag_kernel, out_shape=jax.ShapeDtypeStruct((n, n), F32),...  97.9 us
    dynamic_update_slice x36, local copies, waits for them, and re-layouts, gather(): lax.dynamic_update_slice(out, send(x, m) if m else x, ((me ^ m) * x.shape...  32.9 us
    dynamic_update_slice x20, local copies, waits for them, and re-layouts, local_fit(): col = lax.dynamic_update_slice(col, got[c][m], (0, (tp ^ m) * width))  26.3 us
    dot_general x10, matrix products, local_fit(): jnp.dot(inverses[k], block, precision=HIGHEST, preferred_element_type=F32)  21 us
  transfers between devices with their start and end apart: 73, of which 33 were waited for; matrix products, arithmetic and copies ran while one was open for 26% of the time, Pallas kernels for 8%

profile of v1, /device:TPU:0, one launch (start us, length us, event | category | flops | bytes accessed | tf_op | source)
XLA Modules:
  0.0 977.4 jit_solution(8828919825808979858)
XLA Ops:
  33.3 20.6 %collective-permute-done = f32[1536,128]{1,0:T(8,128)} collective-permute-done((f32[1536,128]{1,0:T(8,128)}, f32[1536,128]{1,0:T(8,128)}, u32[]{:S(2)}, u32[]{:S(2)}) %collective-permute-start) | collective-permute-done | bytes 786464 | tf_op jit(solution)/shard_map/ppermute | solution.py:212
  59.2 10.7 %collective-permute-done.3 = f32[1536,128]{1,0:T(8,128)} collective-permute-done((f32[1536,128]{1,0:T(8,128)}, f32[1536,128]{1,0:T(8,128)}, u32[]{:S(2)}, u32[]{:S(2)}) %collective-permute-start.3) | collective-permute-done | bytes 786464 | tf_op jit(solution)/shard_map/ppermute | solution.py:212
  73.2 69.4 %collective-permute-done.4 = f32[1536,128]{1,0:T(8,128)} collective-permute-done((f32[1536,128]{1,0:T(8,128)}, f32[1536,128]{1,0:T(8,128)}, u32[]{:S(2)}, u32[]{:S(2)}) %collective-permute-start.4) | collective-permute-done | bytes 786464 | tf_op jit(solution)/shard_map/ppermute | solution.py:212
  153.2 12.5 %fusion.50 = f32[512,512]{1,0:T(8,128)} fusion(f32[1536,512]{1,0:T(8,128)S(1)} %constant_dynamic-update-slice_fusion.57, f32[1536,512]{1,0:T(8,128)} %constant_dynamic-update-slice_fusion.52), kind=kOutput, calls=%fused_computation.194 | convolution fusion | flops 4831838208 | bytes 7340032 | tf_op jit(solution)/shard_map/dot_general | solution.py:205
  165.7 13.7 %fusion.51 = f32[512,512]{1,0:T(8,128)} fusion(f32[1536,512]{1,0:T(8,128)} %constant_dynamic-update-slice_fusion.52), kind=kOutput, calls=%fused_computation.195 | convolution fusion | flops 4831838208 | bytes 4194304 | tf_op jit(solution)/shard_map/dot_general | solution.py:205
  205.6 25.7 %collective-permute-done.20 = f32[1536,128]{1,0:T(8,128)S(1)} collective-permute-done((f32[1536,128]{1,0:T(8,128)S(1)}, f32[1536,128]{1,0:T(8,128)S(1)}, u32[]{:S(2)}, u32[]{:S(2)}) %collective-permute-start.20) | collective-permute-done | bytes 786464 | tf_op jit(solution)/shard_map/ppermute | solution.py:212
  232.1 19.3 %collective-permute-done.21 = f32[1536,128]{1,0:T(8,128)S(1)} collective-permute-done((f32[1536,128]{1,0:T(8,128)S(1)}, f32[1536,128]{1,0:T(8,128)S(1)}, u32[]{:S(2)}, u32[]{:S(2)}) %collective-permute-start.21) | collective-permute-done | bytes 786464 | tf_op jit(solution)/shard_map/ppermute | solution.py:212
  272.7 49.9 %collective-permute-start.10 = (f32[48,512]{1,0:T(8,128)S(1)}, f32[48,512]{1,0:T(8,128)S(1)}, u32[]{:S(2)}, u32[]{:S(2)}) collective-permute-start(f32[48,512]{1,0:T(8,128)S(1)} %get-tuple-element.65), channel_id=1, source_target_pairs={{0,8},{8,0},{16,24},{24,16},{1,9},{9,1},{17,25},{25,17},{2,10},{10... | collective-permute-start | bytes 294920 | tf_op jit(solution)/shard_map/ppermute | solution.py:212
  327.5 13.7 %collective-permute-done.11 = f32[48,512]{1,0:T(8,128)S(1)} collective-permute-done((f32[48,512]{1,0:T(8,128)S(1)}, f32[48,512]{1,0:T(8,128)S(1)}, u32[]{:S(2)}, u32[]{:S(2)}) %collective-permute-start.11) | collective-permute-done | bytes 98336 | tf_op jit(solution)/shard_map/ppermute | solution.py:212
  341.2 29.8 %collective-permute-start.56 = (f32[1536,128]{1,0:T(8,128)}, f32[1536,128]{1,0:T(8,128)}, u32[]{:S(2)}, u32[]{:S(2)}) collective-permute-start(f32[1536,128]{1,0:T(8,128)} %get-tuple-element.27), channel_id=1, source_target_pairs={{0,24},{8,16},{16,8},{24,0},{1,25},{9,17},{17,9},{25,1},{2,26},{10... | collective-permute-start | bytes 2359304 | tf_op jit(solution)/shard_map/ppermute | solution.py:212
  468.5 12.6 %fusion.55 = f32[512,512]{1,0:T(8,128)} fusion(f32[1536,512]{1,0:T(8,128)S(1)} %constant_dynamic-update-slice_fusion.57, f32[1536,512]{1,0:T(8,128)} %constant_dynamic-update-slice_fusion.23), kind=kOutput, calls=%fused_computation.199 | convolution fusion | flops 4831838208 | bytes 7340032 | tf_op jit(solution)/shard_map/dot_general | solution.py:205
  481.0 13.7 %fusion.58 = f32[512,512]{1,0:T(8,128)} fusion(f32[1536,512]{1,0:T(8,128)} %constant_dynamic-update-slice_fusion.23), kind=kOutput, calls=%fused_computation.202 | convolution fusion | flops 4831838208 | bytes 4194304 | tf_op jit(solution)/shard_map/dot_general | solution.py:205
  527.4 19.5 %diag_inverse.5.refs_10_ = f32[512,512]{1,0:T(8,128)} custom-call(f32[1]{0:T(128)} %bitcast.288.lam_ref, f32[512,512]{1,0:T(8,128)} %slice.140.s_ref), custom_call_target="tpu_custom_call" | custom-call | flops 20000000000 | bytes 2097152 | tf_op jit(solution)/shard_map/diag_inverse/pallas_call | solution.py:157
  565.7 12.2 %collective-permute-done.34 = f32[192,512]{1,0:T(8,128)S(1)} collective-permute-done((f32[192,512]{1,0:T(8,128)S(1)}, f32[192,512]{1,0:T(8,128)S(1)}, u32[]{:S(2)}, u32[]{:S(2)}) %collective-permute-start.34) | collective-permute-done | bytes 393248 | tf_op jit(solution)/shard_map/ppermute | solution.py:212
  579.5 19.8 %diag_inverse.6.refs_11_ = f32[512,512]{1,0:T(8,128)} custom-call(f32[1]{0:T(128)} %bitcast.289.lam_ref, f32[512,512]{1,0:T(8,128)} %slice_subtract_fusion.12.s_ref), custom_call_target="tpu_custom_call" | custom-call | flops 20000000000 | bytes 2097152 | tf_op jit(solution)/shard_map/diag_inverse/pallas_call | solution.py:157
  623.7 11.0 %collective-permute-done.42 = f32[256,512]{1,0:T(8,128)S(1)} collective-permute-done((f32[256,512]{1,0:T(8,128)S(1)}, f32[256,512]{1,0:T(8,128)S(1)}, u32[]{:S(2)}, u32[]{:S(2)}) %collective-permute-start.42) | collective-permute-done | bytes 524320 | tf_op jit(solution)/shard_map/ppermute | solution.py:212
  661.7 12.7 %convolution_dynamic-update-slice_fusion.3 = f32[2560,512]{1,0:T(8,128)} fusion(f32[1536,512]{1,0:T(8,128)S(1)} %copy-done.30, f32[1536,512]{1,0:T(8,128)} %constant_dynamic-update-slice_fusion.9), kind=kOutput, calls=%fused_computation.15 | convolution fusion | flops 4831838208 | bytes 7340032 | tf_op jit(solution)/shard_map/dot_general | solution.py:205
  678.7 13.6 %convolution_dynamic-update-slice_fusion.2 = f32[2560,512]{1,0:T(8,128)} fusion(f32[2560,512]{1,0:T(8,128)} %convolution_dynamic-update-slice_fusion.3, f32[1536,512]{1,0:T(8,128)} %constant_dynamic-update-slice_fusion.52, f32[1536,512]{1,0:T(8,128)} %constant_dynamic-update-slice_fusion.9), kind=kOutput, calls=%fused_computation.14 | convolution fusion | flops 4831838208 | bytes 7340032 | tf_op jit(solution)/shard_map/dot_general | solution.py:205
  692.4 12.7 %convolution_dynamic-update-slice_fusion.1 = f32[2560,512]{1,0:T(8,128)} fusion(f32[2560,512]{1,0:T(8,128)} %convolution_dynamic-update-slice_fusion.2, f32[1536,512]{1,0:T(8,128)S(1)} %copy-done.33, f32[1536,512]{1,0:T(8,128)} %constant_dynamic-update-slice_fusion.9), kind=kOutput, calls=%fused_computation.13 | convolution fusion | flops 4831838208 | bytes 7340032 | tf_op jit(solution)/shard_map/dot_general | solution.py:205
  705.1 13.7 %convolution_dynamic-update-slice_fusion = f32[2560,512]{1,0:T(8,128)} fusion(f32[2560,512]{1,0:T(8,128)} %convolution_dynamic-update-slice_fusion.1, f32[1536,512]{1,0:T(8,128)} %constant_dynamic-update-slice_fusion.23, f32[1536,512]{1,0:T(8,128)} %constant_dynamic-update-slice_fusion.9), kind=kOutput, calls=%fused_computation.12 | convolution fusion | flops 4831838208 | bytes 7340032 | tf_op jit(solution)/shard_map/dot_general | solution.py:205
  746.2 19.6 %diag_inverse.7.refs_12_ = f32[512,512]{1,0:T(8,128)} custom-call(f32[1]{0:T(128)} %bitcast.290.lam_ref, f32[512,512]{1,0:T(8,128)} %fusion.18.s_ref), custom_call_target="tpu_custom_call" | custom-call | flops 20000000000 | bytes 2097152 | tf_op jit(solution)/shard_map/diag_inverse/pallas_call | solution.py:157
  789.1 13.9 %collective-permute-done.59 = f32[320,512]{1,0:T(8,128)S(1)} collective-permute-done((f32[320,512]{1,0:T(8,128)S(1)}, f32[320,512]{1,0:T(8,128)S(1)}, u32[]{:S(2)}, u32[]{:S(2)}) %collective-permute-start.59) | collective-permute-done | bytes 655392 | tf_op jit(solution)/shard_map/ppermute | solution.py:212
  869.0 19.6 %diag_inverse.8.refs_13_ = f32[512,512]{1,0:T(8,128)} custom-call(f32[1]{0:T(128)} %bitcast.291.lam_ref, f32[512,512]{1,0:T(8,128)} %fusion.8.s_ref), custom_call_target="tpu_custom_call" | custom-call | flops 20000000000 | bytes 2097152 | tf_op jit(solution)/shard_map/diag_inverse/pallas_call | solution.py:157
  922.0 19.4 %diag_inverse.9.refs_14_ = f32[512,512]{1,0:T(8,128)} custom-call(f32[1]{0:T(128)} %bitcast.292.lam_ref, f32[512,512]{1,0:T(8,128)} %fusion.2.s_ref), custom_call_target="tpu_custom_call" | custom-call | flops 20000000000 | bytes 2097152 | tf_op jit(solution)/shard_map/diag_inverse/pallas_call | solution.py:157
  (412 shorter events, 494.9 us)
Async XLA Ops:
  19.8 50.1 %collective-permute-start.3 = (f32[1536,128]{1,0:T(8,128)}, f32[1536,128]{1,0:T(8,128)}, u32[]{:S(2)}, u32[]{:S(2)}) collective-permute-start(f32[1536,128]{1,0:T(8,128)} %get-tuple-element.43), channel_id=1, source_target_pairs={{0,8},{8,0},{16,24},{24,16},{1,9},{9,1},{17,25},{25,17},{2,10},{10... | collective-permute-start | bytes 2359304 | tf_op jit(solution)/shard_map/ppermute | solution.py:212
  19.8 52.2 %collective-permute-start.1 = (f32[1536,128]{1,0:T(8,128)}, f32[1536,128]{1,0:T(8,128)}, u32[]{:S(2)}, u32[]{:S(2)}) collective-permute-start(f32[1536,128]{1,0:T(8,128)} %get-tuple-element.39), channel_id=1, source_target_pairs={{0,16},{8,24},{16,0},{24,8},{1,17},{9,25},{17,1},{25,9},{2,18},{10... | collective-permute-start | bytes 2359304 | tf_op jit(solution)/shard_map/ppermute | solution.py:212
  22.9 121.9 %collective-permute-start.2 = (f32[1536,128]{1,0:T(8,128)}, f32[1536,128]{1,0:T(8,128)}, u32[]{:S(2)}, u32[]{:S(2)}) collective-permute-start(f32[1536,128]{1,0:T(8,128)} %get-tuple-element.38), channel_id=1, source_target_pairs={{0,24},{8,16},{16,8},{24,0},{1,25},{9,17},{17,9},{25,1},{2,26},{10... | collective-permute-start | bytes 2359304 | tf_op jit(solution)/shard_map/ppermute | solution.py:212
  24.2 118.5 %collective-permute-start.4 = (f32[1536,128]{1,0:T(8,128)}, f32[1536,128]{1,0:T(8,128)}, u32[]{:S(2)}, u32[]{:S(2)}) collective-permute-start(f32[1536,128]{1,0:T(8,128)} %get-tuple-element.42), channel_id=1, source_target_pairs={{0,16},{8,24},{16,0},{24,8},{1,17},{9,25},{17,1},{25,9},{2,18},{10... | collective-permute-start | bytes 2359304 | tf_op jit(solution)/shard_map/ppermute | solution.py:212
  53.9 98.3 %collective-permute-start.5 = (f32[1536,128]{1,0:T(8,128)}, f32[1536,128]{1,0:T(8,128)S(1)}, u32[]{:S(2)}, u32[]{:S(2)}) collective-permute-start(f32[1536,128]{1,0:T(8,128)} %get-tuple-element.41), channel_id=1, source_target_pairs={{0,24},{8,16},{16,8},{24,0},{1,25},{9,17},{17,9},{25,1},{2,26},{10... | collective-permute-start | bytes 2359304 | tf_op jit(solution)/shard_map/ppermute | solution.py:212
  188.0 67.4 %collective-permute-start.6 = (f32[768,512]{1,0:T(8,128)S(1)}, f32[768,512]{1,0:T(8,128)S(1)}, u32[]{:S(2)}, u32[]{:S(2)}) collective-permute-start(f32[768,512]{1,0:T(8,128)S(1)} %dynamic-slice_bitcast_fusion.3), channel_id=1, source_target_pairs={{0,1},{1,0},{2,3},{3,2},{4,5},{5,4},{6,7},{7,6},{8,9},{9,8},{10,11... | collective-permute-start | bytes 4718600 | tf_op jit(solution)/shard_map/ppermute | solution.py:212
  196.8 54.7 %collective-permute-start.21 = (f32[1536,128]{1,0:T(8,128)S(1)}, f32[1536,128]{1,0:T(8,128)S(1)}, u32[]{:S(2)}, u32[]{:S(2)}) collective-permute-start(f32[1536,128]{1,0:T(8,128)S(1)} %get-tuple-element.34), channel_id=1, source_target_pairs={{0,16},{8,24},{16,0},{24,8},{1,17},{9,25},{17,1},{25,9},{2,18},{10... | collective-permute-start | bytes 2359304 | tf_op jit(solution)/shard_map/ppermute | solution.py:212
  198.7 53.6 %collective-permute-start.22 = (f32[1536,128]{1,0:T(8,128)S(1)}, f32[1536,128]{1,0:T(8,128)S(1)}, u32[]{:S(2)}, u32[]{:S(2)}) collective-permute-start(f32[1536,128]{1,0:T(8,128)S(1)} %get-tuple-element.33), channel_id=1, source_target_pairs={{0,24},{8,16},{16,8},{24,0},{1,25},{9,17},{17,9},{25,1},{2,26},{10... | collective-permute-start | bytes 2359304 | tf_op jit(solution)/shard_map/ppermute | solution.py:212
  201.4 123.1 %collective-permute-start.37 = (f32[1536,128]{1,0:T(8,128)S(1)}, f32[1536,128]{1,0:T(8,128)S(1)}, u32[]{:S(2)}, u32[]{:S(2)}) collective-permute-start(f32[1536,128]{1,0:T(8,128)S(1)} %get-tuple-element.32), channel_id=1, source_target_pairs={{0,8},{8,0},{16,24},{24,16},{1,9},{9,1},{17,25},{25,17},{2,10},{10... | collective-permute-start | bytes 2359304 | tf_op jit(solution)/shard_map/ppermute | solution.py:212
  231.2 165.6 %collective-permute-start.38 = (f32[1536,128]{1,0:T(8,128)}, f32[1536,128]{1,0:T(8,128)}, u32[]{:S(2)}, u32[]{:S(2)}) collective-permute-start(f32[1536,128]{1,0:T(8,128)} %get-tuple-element.31), channel_id=1, source_target_pairs={{0,16},{8,24},{16,0},{24,8},{1,17},{9,25},{17,1},{25,9},{2,18},{10... | collective-permute-start | bytes 2359304 | tf_op jit(solution)/shard_map/ppermute | solution.py:212
  267.1 132.0 %collective-permute-start.39 = (f32[1536,128]{1,0:T(8,128)}, f32[1536,128]{1,0:T(8,128)}, u32[]{:S(2)}, u32[]{:S(2)}) collective-permute-start(f32[1536,128]{1,0:T(8,128)} %get-tuple-element.30), channel_id=1, source_target_pairs={{0,24},{8,16},{16,8},{24,0},{1,25},{9,17},{17,9},{25,1},{2,26},{10... | collective-permute-start | bytes 2359304 | tf_op jit(solution)/shard_map/ppermute | solution.py:212
  272.7 54.2 %collective-permute-start.10 = (f32[48,512]{1,0:T(8,128)S(1)}, f32[48,512]{1,0:T(8,128)S(1)}, u32[]{:S(2)}, u32[]{:S(2)}) collective-permute-start(f32[48,512]{1,0:T(8,128)S(1)} %get-tuple-element.65), channel_id=1, source_target_pairs={{0,8},{8,0},{16,24},{24,16},{1,9},{9,1},{17,25},{25,17},{2,10},{10... | collective-permute-start | bytes 294920 | tf_op jit(solution)/shard_map/ppermute | solution.py:212
  326.9 74.3 %collective-permute-start.54 = (f32[1536,128]{1,0:T(8,128)}, f32[1536,128]{1,0:T(8,128)}, u32[]{:S(2)}, u32[]{:S(2)}) collective-permute-start(f32[1536,128]{1,0:T(8,128)} %get-tuple-element.29), channel_id=1, source_target_pairs={{0,8},{8,0},{16,24},{24,16},{1,9},{9,1},{17,25},{25,17},{2,10},{10... | collective-permute-start | bytes 2359304 | tf_op jit(solution)/shard_map/ppermute | solution.py:212
  341.2 62.1 %collective-permute-start.55 = (f32[1536,128]{1,0:T(8,128)}, f32[1536,128]{1,0:T(8,128)}, u32[]{:S(2)}, u32[]{:S(2)}) collective-permute-start(f32[1536,128]{1,0:T(8,128)} %get-tuple-element.28), channel_id=1, source_target_pairs={{0,16},{8,24},{16,0},{24,8},{1,17},{9,25},{17,1},{25,9},{2,18},{10... | collective-permute-start | bytes 2359304 | tf_op jit(solution)/shard_map/ppermute | solution.py:212
  341.2 66.0 %collective-permute-start.56 = (f32[1536,128]{1,0:T(8,128)}, f32[1536,128]{1,0:T(8,128)}, u32[]{:S(2)}, u32[]{:S(2)}) collective-permute-start(f32[1536,128]{1,0:T(8,128)} %get-tuple-element.27), channel_id=1, source_target_pairs={{0,24},{8,16},{16,8},{24,0},{1,25},{9,17},{17,9},{25,1},{2,26},{10... | collective-permute-start | bytes 2359304 | tf_op jit(solution)/shard_map/ppermute | solution.py:212
  444.2 77.8 %collective-permute-start.19 = (f32[768,512]{1,0:T(8,128)}, f32[768,512]{1,0:T(8,128)}, u32[]{:S(2)}, u32[]{:S(2)}) collective-permute-start(f32[768,512]{1,0:T(8,128)} %constant_dynamic-update-slice_fusion.43), channel_id=1, source_target_pairs={{0,1},{1,0},{2,3},{3,2},{4,5},{5,4},{6,7},{7,6},{8,9},{9,8},{10,11... | collective-permute-start | bytes 4718600 | tf_op jit(solution)/shard_map/ppermute | solution.py:212
  494.7 55.6 %collective-permute-start.30 = (f32[48,512]{1,0:T(8,128)}, f32[48,512]{1,0:T(8,128)}, u32[]{:S(2)}, u32[]{:S(2)}) collective-permute-start(f32[48,512]{1,0:T(8,128)} %get-tuple-element.19), channel_id=1, source_target_pairs={{0,8},{8,0},{16,24},{24,16},{1,9},{9,1},{17,25},{25,17},{2,10},{10... | collective-permute-start | bytes 294920 | tf_op jit(solution)/shard_map/ppermute | solution.py:212
  496.4 54.8 %collective-permute-start.31 = (f32[48,512]{1,0:T(8,128)}, f32[48,512]{1,0:T(8,128)}, u32[]{:S(2)}, u32[]{:S(2)}) collective-permute-start(f32[48,512]{1,0:T(8,128)} %get-tuple-element.19), channel_id=1, source_target_pairs={{0,16},{8,24},{16,0},{24,8},{1,17},{9,25},{17,1},{25,9},{2,18},{10... | collective-permute-start | bytes 294920 | tf_op jit(solution)/shard_map/ppermute | solution.py:212
  497.8 54.3 %collective-permute-start.32 = (f32[48,512]{1,0:T(8,128)}, f32[48,512]{1,0:T(8,128)}, u32[]{:S(2)}, u32[]{:S(2)}) collective-permute-start(f32[48,512]{1,0:T(8,128)} %get-tuple-element.19), channel_id=1, source_target_pairs={{0,24},{8,16},{16,8},{24,0},{1,25},{9,17},{17,9},{25,1},{2,26},{10... | collective-permute-start | bytes 294920 | tf_op jit(solution)/shard_map/ppermute | solution.py:212
  522.0 84.6 %collective-permute-start.40 = (f32[1024,512]{1,0:T(8,128)}, f32[1024,512]{1,0:T(8,128)}, u32[]{:S(2)}, u32[]{:S(2)}) collective-permute-start(f32[1024,512]{1,0:T(8,128)} %dynamic-slice_bitcast_fusion.1), channel_id=1, source_target_pairs={{0,1},{1,0},{2,3},{3,2},{4,5},{5,4},{6,7},{7,6},{8,9},{9,8},{10,11... | collective-permute-start | bytes 6291464 | tf_op jit(solution)/shard_map/ppermute | solution.py:212
  674.3 45.5 %collective-permute-start.47 = (f32[64,512]{1,0:T(8,128)}, f32[64,512]{1,0:T(8,128)S(1)}, u32[]{:S(2)}, u32[]{:S(2)}) collective-permute-start(f32[64,512]{1,0:T(8,128)} %get-tuple-element.17), channel_id=1, source_target_pairs={{0,8},{8,0},{16,24},{24,16},{1,9},{9,1},{17,25},{25,17},{2,10},{10... | collective-permute-start | bytes 393224 | tf_op jit(solution)/shard_map/ppermute | solution.py:212
  676.3 43.6 %collective-permute-start.48 = (f32[64,512]{1,0:T(8,128)}, f32[64,512]{1,0:T(8,128)S(1)}, u32[]{:S(2)}, u32[]{:S(2)}) collective-permute-start(f32[64,512]{1,0:T(8,128)} %get-tuple-element.17), channel_id=1, source_target_pairs={{0,16},{8,24},{16,0},{24,8},{1,17},{9,25},{17,1},{25,9},{2,18},{10... | collective-permute-start | bytes 393224 | tf_op jit(solution)/shard_map/ppermute | solution.py:212
  677.3 42.6 %collective-permute-start.49 = (f32[64,512]{1,0:T(8,128)}, f32[64,512]{1,0:T(8,128)S(1)}, u32[]{:S(2)}, u32[]{:S(2)}) collective-permute-start(f32[64,512]{1,0:T(8,128)} %get-tuple-element.17), channel_id=1, source_target_pairs={{0,24},{8,16},{16,8},{24,0},{1,25},{9,17},{17,9},{25,1},{2,26},{10... | collective-permute-start | bytes 393224 | tf_op jit(solution)/shard_map/ppermute | solution.py:212
  725.4 42.7 %collective-permute-start.57 = (f32[1280,512]{1,0:T(8,128)}, f32[1280,512]{1,0:T(8,128)}, u32[]{:S(2)}, u32[]{:S(2)}) collective-permute-start(f32[1280,512]{1,0:T(8,128)} %dynamic-slice_bitcast_fusion), channel_id=1, source_target_pairs={{0,1},{1,0},{2,3},{3,2},{4,5},{5,4},{6,7},{7,6},{8,9},{9,8},{10,11... | collective-permute-start | bytes 7864328 | tf_op jit(solution)/shard_map/ppermute | solution.py:212
  (98 other events, 1810.1 us)
